TPU v7x, 32 devices: a whole 2x2x4 slice. The times are simulated.
32 devices in a mesh: src: 8 (over z, x), tgt: 4 (over y, core).
Axes of the slice: x: 2, y: 2, z: 4, core: 2. Of those that a mesh axis runs over, the one named last changes fastest.
Arguments:
- sources: bfloat16 [65536, 64], P(('src', 'tgt')), may hold values from -2.09375 to 2.09375
- targets: bfloat16 [65536, 64], P('tgt'), may hold values from -2.09375 to 2.09375
- potential: float32 [65536], P('src'), may hold values from -1 to 112
- block_map: int32 [256, 20], P('src'), may hold values from -1 to 255, as said below
- counts: int32 [256], P('src'), may hold values from 10 to 20, as said below
- step_history: float32 [8, 65536], P(None, ('src', 'tgt')), may hold values from -13 to 13
- slope_history: float32 [8, 65536], P(None, ('src', 'tgt')), may hold values from -64 to 64, as said below
Outputs:
- gradient: float32 [65536], P(('src', 'tgt'))
- direction: float32 [65536], P(('src', 'tgt'))
- target_potential: float32 [65536], P('tgt')
Inputs may be any that keep to these rules, and one draw needn't show every extreme that they name: `block_map`: row b lists counts[b] different target block numbers in slots 0 to counts[b] - 1 and -1 in the other slots; every target block is listed in some row. `counts`: some source block lists exactly 20 target blocks in every draw. For every k the sum over all points of step_history[k] slope_history[k] is positive.
All inputs are finite; a program needn't handle non-finite values.
Results may differ from a plain program's by a relative error of at most 0.0008.
Values may be sent and summed in bfloat16 or wider, within the bound.
A program may use at most 64 MiB of HBM per device.

v0:
```python
import jax
import jax.numpy as jnp
from jax import lax
from jax.sharding import PartitionSpec as P

BLOCK = 256
entropy = 0.5
tile_group = 16


def merged(part, axis, combine):
    gathered = jax.tree.map(lambda a: lax.all_gather(a, axis), part)

    def take(source):
        return jax.tree.map(lambda a: lax.dynamic_index_in_dim(a, source, 0, False), gathered)

    return lax.fori_loop(
        1, lax.axis_size(axis), lambda source, state: combine(state, take(source)), take(0)
    )


def combine_columns(earlier, later):
    peak = jnp.maximum(earlier[0], later[0])
    return (peak, earlier[1] * jnp.exp(earlier[0] - peak) + later[1] * jnp.exp(later[0] - peak))


def pair_scores(source_tiles, potential_tiles, target_tiles, source_ids, target_ids):
    rows_in = source_tiles[source_ids]
    columns_in = target_tiles[target_ids]
    product = jnp.einsum("gid,gjd->gij", rows_in, columns_in, preferred_element_type=jnp.float32)
    return (potential_tiles[source_ids][:, :, None] + product) / entropy


def upper_solve(upper, right_side, stored):
    values = [None] * stored
    for row in reversed(range(stored)):
        accum = right_side[row]
        for other in range(row + 1, stored):
            accum = accum - upper[row, other] * values[other]
        values[row] = accum / upper[row, row]
    return jnp.stack(values)


def lower_solve(upper, right_side, stored):
    values = [None] * stored
    for row in range(stored):
        accum = right_side[row]
        for other in range(row):
            accum = accum - upper[other, row] * values[other]
        values[row] = accum / upper[row, row]
    return jnp.stack(values)


def per_device(sources, targets, potential, block_map, counts, step_history, slope_history):
    gathered = lax.all_gather(sources, "tgt", axis=0, tiled=True)
    features = gathered.shape[1]
    source_blocks = gathered.shape[0] // BLOCK
    target_blocks = targets.shape[0] // BLOCK
    listed = block_map.shape[1]
    source_tiles = gathered.reshape(source_blocks, BLOCK, features)
    target_tiles = targets.reshape(target_blocks, BLOCK, features)
    potential_tiles = potential.reshape(source_blocks, BLOCK)
    column_rank = lax.axis_index("tgt")
    slot_index = jnp.arange(listed, dtype=jnp.int32)
    owned = (slot_index[None, :] < counts[:, None]) & (block_map // target_blocks == column_rank)
    flat_owned = owned.reshape(-1)
    slot_total = source_blocks * listed
    padded_total = -(-slot_total // tile_group) * tile_group
    flat_index = jnp.arange(slot_total, dtype=jnp.int32)
    ordering = jnp.argsort(jnp.where(flat_owned, 0, slot_total) + flat_index)
    ordering = jnp.concatenate([ordering, jnp.zeros((padded_total - slot_total,), jnp.int32)])
    pair_total = jnp.sum(flat_owned.astype(jnp.int32))
    live_pairs = jnp.arange(padded_total, dtype=jnp.int32) < pair_total
    source_list = jnp.where(live_pairs, ordering // listed, 0)
    target_list = jnp.where(
        live_pairs, block_map.reshape(-1)[ordering] - column_rank * target_blocks, target_blocks
    )
    turn_count = (pair_total + tile_group - 1) // tile_group

    def group_of(turn_index):
        offset = turn_index * tile_group
        source_ids = lax.dynamic_slice_in_dim(source_list, offset, tile_group)
        target_ids = lax.dynamic_slice_in_dim(target_list, offset, tile_group)
        live = lax.dynamic_slice_in_dim(live_pairs, offset, tile_group)
        clipped = jnp.minimum(target_ids, target_blocks - 1)
        scores = pair_scores(source_tiles, potential_tiles, target_tiles, source_ids, clipped)
        return (scores, source_ids, target_ids, clipped, live)

    def column_turn(turn_index, carry):
        peak, total = carry
        scores, source_ids, target_ids, clipped, live = group_of(turn_index)
        tile_peak = jnp.max(scores, axis=1)
        tile_total = jnp.sum(jnp.exp(scores - tile_peak[:, None, :]), axis=1)
        new_peak = peak.at[target_ids].max(tile_peak)
        total = total * jnp.exp(peak - new_peak)
        total = total.at[target_ids].add(tile_total * jnp.exp(tile_peak - new_peak[target_ids]))
        return (new_peak, total)

    start_peak = jnp.full((target_blocks + 1, BLOCK), -1e30, jnp.float32)
    start_total = jnp.zeros((target_blocks + 1, BLOCK), jnp.float32)
    peak, total = lax.fori_loop(0, turn_count, column_turn, (start_peak, start_total))
    local_peak = peak[:target_blocks].reshape(-1)
    local_total = total[:target_blocks].reshape(-1)
    merged_peak, merged_total = merged((local_peak, local_total), "src", combine_columns)
    logs = merged_peak + jnp.log(merged_total)
    target_potential = -entropy * logs
    log_tiles = logs.reshape(target_blocks, BLOCK)

    def row_turn(turn_index, masses):
        scores, source_ids, target_ids, clipped, live = group_of(turn_index)
        weights = jnp.exp(scores - log_tiles[clipped][:, None, :])
        row_sums = jnp.where(live[:, None], jnp.sum(weights, axis=2), 0.0)
        return masses.at[source_ids].add(row_sums)

    masses = lax.fori_loop(0, turn_count, row_turn, jnp.zeros((source_blocks, BLOCK), jnp.float32))
    row_total = lax.psum_scatter(masses.reshape(-1), "tgt", scatter_dimension=0, tiled=True)
    ratio = source_blocks * lax.axis_size("src") / (target_blocks * lax.axis_size("tgt"))
    gradient = 1.0 - ratio * row_total
    stored = step_history.shape[0]
    highest = lax.Precision.HIGHEST
    cross_local = jnp.dot(step_history, slope_history.T, precision=highest)
    slope_local = jnp.dot(slope_history, slope_history.T, precision=highest)
    step_grad = jnp.dot(step_history, gradient, precision=highest)
    slope_grad = jnp.dot(slope_history, gradient, precision=highest)
    cross, slopes, step_dots, slope_dots = lax.psum(
        (cross_local, slope_local, step_grad, slope_grad), ("src", "tgt")
    )
    diagonal = jnp.diag(cross)
    scale = cross[stored - 1, stored - 1] / slopes[stored - 1, stored - 1]
    first_solve = upper_solve(cross, step_dots, stored)
    right_side = (
        diagonal * first_solve
        + scale * jnp.dot(slopes, first_solve, precision=highest)
        - scale * slope_dots
    )
    second_solve = lower_solve(cross, right_side, stored)
    result = (
        scale * gradient
        + jnp.dot(second_solve, step_history, precision=highest)
        - scale * jnp.dot(first_solve, slope_history, precision=highest)
    )
    direction = -result
    return (gradient, direction, target_potential)


def solution(mesh):
    in_specs = (
        P(("src", "tgt"), None),
        P("tgt", None),
        P("src"),
        P("src", None),
        P("src"),
        P(None, ("src", "tgt")),
        P(None, ("src", "tgt")),
    )
    out_specs = (P(("src", "tgt")), P(("src", "tgt")), P("tgt"))
    return jax.shard_map(
        per_device, mesh=mesh, in_specs=in_specs, out_specs=out_specs, check_vma=False
    )
```

profile of v0, /device:TPU:0, one launch (start us, length us, event | category | flops | bytes accessed | tf_op | source)
XLA Modules:
  0.0 390.4 jit_solution(8471207344332975932)
XLA Ops:
  9.9 0.8 copy.30
  11.1 4.8 %copy.31 = bf16[16384,64]{1,0:T(8,128)(2,1)} copy(bf16[16384,64]{0,1:T(8,128)(2,1)} %param.14) | data formatting | bytes 4194304 | tf_op args[1]
  15.9 4.4 %sort.17 = (s32[640]{0:T(1024)}, s32[640]{0:T(1024)S(1)}) sort(s32[640]{0:T(1024)S(1)} %iota_add_fusion, s32[640]{0:T(1024)S(1)} %iota.27), dimensions={0}, to_apply=%region_1.2 | sort | flops 6400 | bytes 10240 | tf_op jit(solution)/shard_map/jit(argsort)/sort | solution.py:70
  21.0 2.8 gather_fusion.7
  26.8 3.8 all-gather.4.cloned.1.call-done
  30.6 2.0 copy.29
  32.7 84.1 %while.39 = (s32[]{:T(128)}, f32[65,256]{1,0:T(8,128)S(1)}, f32[65,256]{1,0:T(8,128)S(1)}, s32[]{:T(128)}, s32[640]{0:T(1024)S(1)}, /*index=5*/s32[640]{0:T(1024...) while((s32[]{:T(128)}, f32[65,256]{1,0:T(8,128)S(1)}, ...), condition=%wide.region_7.8_spmd, body=%wide.region_2.7_spmd.sunk | while | flops 141602464 | bytes 20809704 | solution.py:101
  34.2 2.9 gather_fusion.2
  37.1 1.4 fusion.56
  38.5 1.1 exponential_reduce_fusion.4
  42.6 2.9 gather_fusion.2
  45.5 1.3 fusion.56
  46.9 1.1 exponential_reduce_fusion.4
  51.0 2.9 gather_fusion.2
  53.9 1.3 fusion.56
  55.3 1.1 exponential_reduce_fusion.4
  59.4 2.9 gather_fusion.2
  62.3 1.3 fusion.56
  63.7 1.1 exponential_reduce_fusion.4
  67.8 2.9 gather_fusion.2
  70.7 1.3 fusion.56
  72.1 1.1 exponential_reduce_fusion.4
  76.2 2.9 gather_fusion.2
  79.1 1.4 fusion.56
  80.5 1.1 exponential_reduce_fusion.4
  84.6 2.9 gather_fusion.2
  87.6 1.3 fusion.56
  88.9 1.1 exponential_reduce_fusion.4
  93.0 2.9 gather_fusion.2
  96.0 1.4 fusion.56
  97.3 1.1 exponential_reduce_fusion.4
  101.4 2.9 gather_fusion.2
  104.4 1.4 fusion.56
  105.8 1.1 exponential_reduce_fusion.4
  109.9 2.9 gather_fusion.2
  112.8 1.3 fusion.56
  114.2 1.1 exponential_reduce_fusion.4
  116.9 31.7 %all-gather = f32[8,1,16384]{2,1,0:T(1,128)S(1)} all-gather(f32[1,1,16384]{2,1,0:T(1,128)S(1)} %reshape.154), channel_id=1, replica_groups=mesh['src'=8,'tgt'=4] {'src'}, dimensions={0}, use_global_device_ids=true | all-gather | bytes 589824 | tf_op jit(solution)/shard_map/all_gather | solution.py:12
  149.0 31.7 %all-gather.1 = f32[8,1,16384]{2,1,0:T(1,128)S(1)} all-gather(f32[1,1,16384]{2,1,0:T(1,128)S(1)} %reshape.156), channel_id=1, replica_groups=mesh['src'=8,'tgt'=4] {'src'}, dimensions={0}, use_global_device_ids=true | all-gather | bytes 589824 | tf_op jit(solution)/shard_map/all_gather | solution.py:12
  181.1 1.4 while.40
  183.1 90.2 %while.41 = (s32[]{:T(128)}, f32[32,256]{1,0:T(8,128)S(1)}, s32[]{:T(128)}, s32[640]{0:T(1024)S(1)}, pred[640]{0:T(1024)(128)(4,1)S(1)}, /*index=5*/f32[32,256]{...) while((s32[]{:T(128)}, f32[32,256]{1,0:T(8,128)S(1)}, ...), condition=%wide.region_13.14_spmd, body=%wide.region_10.13_spmd.sunk | while | flops 138418288 | bytes 3319143 | solution.py:115
  184.6 3.8 gather_fusion.4
  189.0 2.3 exponential_reduce_fusion.5
  193.6 3.8 gather_fusion.4
  198.0 2.3 exponential_reduce_fusion.5
  202.6 3.8 gather_fusion.4
  207.0 2.3 exponential_reduce_fusion.5
  209.4 0.8 scatter_custom_fusion.14
  211.6 3.8 gather_fusion.4
  216.1 2.3 exponential_reduce_fusion.5
  220.6 3.8 gather_fusion.4
  225.1 2.3 exponential_reduce_fusion.5
  229.7 3.8 gather_fusion.4
  234.1 2.3 exponential_reduce_fusion.5
  238.7 3.8 gather_fusion.4
  243.1 2.3 exponential_reduce_fusion.5
  247.7 3.8 gather_fusion.4
  252.1 2.3 exponential_reduce_fusion.5
  256.7 3.8 gather_fusion.4
  261.1 2.3 exponential_reduce_fusion.5
  265.7 3.8 gather_fusion.4
  270.1 2.3 exponential_reduce_fusion.5
  273.3 10.3 %all-reduce = f32[8192]{0:T(1024)S(1)} all-reduce(f32[8192]{0:T(1024)S(1)} %bitcast.147), channel_id=2, replica_groups=mesh['src'=8,'tgt'=4] {'tgt'}, use_global_device_ids=true, to_apply=%region_14.15.clone | all-reduce | flops 8192 | bytes 65536
  284.2 37.0 %all-reduce.1 = (f32[8]{0:T(128)S(1)}, f32[8,8]{1,0:T(8,128)S(1)}, f32[8,8]{1,0:T(8,128)S(1)}, f32[8]{0:T(128)S(1)}) all-reduce(f32[8]{0:T(128)S(1)} %convolution_bitcast_fusion.2, f32[8,8]{1,0:T(8,128)S(1)} %fusion.29, f32[8,8]{1,0:T(8,128)S(1)} %fusion.30, ...), channel_id=1, replica_groups=mesh['src'=8,'tgt'=4] {'src','tgt'}, use_global_device_ids=true, to_apply=%region_17.18 | all-reduce | flops 144 | bytes 1152 | tf_op jit(solution)/shard_map/psum | solution.py:125
  (300 shorter events, 70.6 us)
Async XLA Ops:
  7.2 19.2 %copy-start = (f32[8,2048]{1,0:T(8,128)S(1)}, f32[8,2048]{1,0:T(8,128)}, u32[]{:S(2)}) copy-start(f32[8,2048]{1,0:T(8,128)} %param.19) | copy-start | bytes 196612
  7.2 8.7 %copy-start.5 = (f32[8192]{0:T(1024)S(1)}, f32[8192]{0:T(1024)}, u32[]{:S(2)}) copy-start(f32[8192]{0:T(1024)} %param.15) | copy-start | bytes 98308
  7.2 23.4 %all-gather.4.cloned.1.call-start = ((), (), s32[]{:S(2)}) async-start(), calls=%async_computation | async-start | bytes 1310720 | tf_op jit(solution)/shard_map/all_gather | solution.py:55
  11.0 12.8 %copy-start.6 = (u32[32]{0:T(128)S(1)}, u32[32]{0:T(128)}, u32[]{:S(2)}) copy-start(u32[32]{0:T(128)} %constant.169) | copy-start | bytes 388
  11.0 15.5 %copy-start.3 = (f32[8,2048]{1,0:T(8,128)S(1)}, f32[8,2048]{1,0:T(8,128)}, u32[]{:S(2)}) copy-start(f32[8,2048]{1,0:T(8,128)} %param.18) | copy-start | bytes 196612
  32.7 1.5 copy-start.1
  38.5 2.6 copy-start.2
  41.1 1.5 copy-start.1
  46.9 2.6 copy-start.2
  49.5 1.5 copy-start.1
  55.3 2.6 copy-start.2
  57.9 1.5 copy-start.1
  63.7 2.6 copy-start.2
  66.3 1.5 copy-start.1
  72.1 2.6 copy-start.2
  74.7 1.5 copy-start.1
  80.5 2.6 copy-start.2
  83.2 1.5 copy-start.1
  88.9 2.6 copy-start.2
  91.6 1.5 copy-start.1
  97.3 2.6 copy-start.2
  100.0 1.5 copy-start.1
  105.7 2.6 copy-start.2
  108.4 1.5 copy-start.1
  114.2 2.6 copy-start.2
  283.6 100.0 %copy-start.4 = (f32[2048]{0:T(1024)}, f32[2048]{0:T(1024)S(1)}, u32[]{:S(2)}) copy-start(f32[2048]{0:T(1024)S(1)} %dynamic-slice_subtract_fusion) | copy-start | bytes 24580
Sparse Core Ops, SparseCore 0:
  9.6 21.0 all-gather.3
where the time goes:
time: 393 us; the launch traced here: 390 us
  local copies, waits for them, and re-layouts  118 us (30%)
  blocking collectives  111 us (28%)
  between operations  72.7 us (18%)
  other arithmetic  44.5 us (11%)
  matrix products  37.6 us (10%)
  waiting for transfers between devices  4.5 us (1%)
    gather x20, local copies, waits for them, and re-layouts, pair_scores(): columns_in = target_tiles[target_ids]  67.8 us
    all_gather x2, blocking collectives, merged(): gathered = jax.tree.map(lambda a: lax.all_gather(a, axis), part)  63.4 us
    psum x1, blocking collectives, per_device(): lax.psum((cross_local, slope_local, step_grad, slope_grad), ('src', 'tgt'))  37 us
    dot_general x20, matrix products, pair_scores(): jnp.einsum('gid,gjd->gij', rows_in, columns_in, preferred_element_type=jn...  36.1 us
    gather x20, local copies, waits for them, and re-layouts, pair_scores(): rows_in = source_tiles[source_ids]  15 us
    gather x20, local copies, waits for them, and re-layouts, pair_scores(): return (potential_tiles[source_ids][:, :, None] + product) / entropy  11.5 us
    reduce_sum x10, other arithmetic, column_turn(): tile_total = jnp.sum(jnp.exp(scores - tile_peak[:, None, :]), axis=1)  10.8 us
    unnamed x1, blocking collectives  10.3 us
  transfers between devices with their start and end apart: 1, of which 1 were waited for; matrix products, arithmetic and copies ran while one was open for 4% of the time, Pallas kernels for 0%

commit v1 on v0

--- a/solution.py
+++ b/solution.py
@@ -123,7 +123,7 @@
     step_grad = jnp.dot(step_history, gradient, precision=highest)
     slope_grad = jnp.dot(slope_history, gradient, precision=highest)
     cross, slopes, step_dots, slope_dots = lax.psum(
-        (cross_local, slope_local, step_grad, slope_grad), ("src", "tgt")
+        lax.psum((cross_local, slope_local, step_grad, slope_grad), "tgt"), "src"
     )
     diagonal = jnp.diag(cross)
     scale = cross[stored - 1, stored - 1] / slopes[stored - 1, stored - 1]

time: 393 us -> 379 us (0.964)
  blocking collectives: 111 us -> 97.3 us
    psum x1 -> x2, blocking collectives: 37 us -> 23.6 us  [the longest x1 17.6 us: per_device(): lax.psum(lax.psum((cross_local, slope_local, step_grad, slope_grad), 'tgt...]
  transfers between devices with their start and end apart: 1 -> 1, of which waited for: 1 -> 1; matrix products, arithmetic and copies ran while one was open for 4% -> 5% of each run, Pallas kernels for 0% -> 0%
where the time goes in v1:
time: 379 us; the launch traced here: 377 us
  local copies, waits for them, and re-layouts  118 us (31%)
  blocking collectives  97.3 us (26%)
  between operations  72.7 us (19%)
  other arithmetic  44.5 us (12%)
  matrix products  37.6 us (10%)
  waiting for transfers between devices  4.5 us (1%)
    gather x20, local copies, waits for them, and re-layouts, pair_scores(): columns_in = target_tiles[target_ids]  67.8 us
    all_gather x2, blocking collectives, merged(): gathered = jax.tree.map(lambda a: lax.all_gather(a, axis), part)  63.4 us
    dot_general x20, matrix products, pair_scores(): jnp.einsum('gid,gjd->gij', rows_in, columns_in, preferred_element_type=jn...  36.1 us
    psum x1, blocking collectives, per_device(): lax.psum(lax.psum((cross_local, slope_local, step_grad, slope_grad), 'tgt...  17.6 us
    gather x20, local copies, waits for them, and re-layouts, pair_scores(): rows_in = source_tiles[source_ids]  15 us
    gather x20, local copies, waits for them, and re-layouts, pair_scores(): return (potential_tiles[source_ids][:, :, None] + product) / entropy  11.5 us
    reduce_sum x10, other arithmetic, column_turn(): tile_total = jnp.sum(jnp.exp(scores - tile_peak[:, None, :]), axis=1)  10.8 us
    unnamed x1, blocking collectives  10.3 us
  transfers between devices with their start and end apart: 1, of which 1 were waited for; matrix products, arithmetic and copies ran while one was open for 5% of the time, Pallas kernels for 0%

profile of v1, /device:TPU:0, one launch (start us, length us, event | category | flops | bytes accessed | tf_op | source)
XLA Modules:
  0.0 377.1 jit_solution(15358700447379526323)
XLA Ops:
  9.9 0.8 copy.30
  11.1 4.8 %copy.31 = bf16[16384,64]{1,0:T(8,128)(2,1)} copy(bf16[16384,64]{0,1:T(8,128)(2,1)} %param.14) | data formatting | bytes 4194304 | tf_op args[1]
  15.9 4.4 %sort.17 = (s32[640]{0:T(1024)}, s32[640]{0:T(1024)S(1)}) sort(s32[640]{0:T(1024)S(1)} %iota_add_fusion, s32[640]{0:T(1024)S(1)} %iota.27), dimensions={0}, to_apply=%region_1.2 | sort | flops 6400 | bytes 10240 | tf_op jit(solution)/shard_map/jit(argsort)/sort | solution.py:70
  21.0 2.8 gather_fusion.7
  26.8 3.8 %all-gather.4.cloned.1.call-done = bf16[8192,64]{0,1:T(8,128)(2,1)} async-done(((bf16[2048,64]{0,1:T(8,128)(2,1)}), bf16[8192,64]{0,1:T(8,128)(2,1)}) %all-gather.4.cloned.1.call-update) | async-done | bytes 1048592 | tf_op jit(solution)/shard_map/all_gather | solution.py:55
  30.6 2.0 copy.29
  32.7 84.1 %while.39 = (s32[]{:T(128)}, f32[65,256]{1,0:T(8,128)S(1)}, f32[65,256]{1,0:T(8,128)S(1)}, s32[]{:T(128)}, s32[640]{0:T(1024)S(1)}, /*index=5*/s32[640]{0:T(1024...) while((s32[]{:T(128)}, f32[65,256]{1,0:T(8,128)S(1)}, ...), condition=%wide.region_7.8_spmd, body=%wide.region_2.7_spmd.sunk | while | flops 141602464 | bytes 20809704 | solution.py:101
  34.2 2.9 gather_fusion.2
  37.1 1.4 fusion.56
  38.5 1.1 exponential_reduce_fusion.4
  42.6 2.9 gather_fusion.2
  45.5 1.3 fusion.56
  46.9 1.1 exponential_reduce_fusion.4
  51.0 2.9 gather_fusion.2
  53.9 1.3 fusion.56
  55.3 1.1 exponential_reduce_fusion.4
  59.4 2.9 gather_fusion.2
  62.3 1.3 fusion.56
  63.7 1.1 exponential_reduce_fusion.4
  67.8 2.9 gather_fusion.2
  70.7 1.3 fusion.56
  72.1 1.1 exponential_reduce_fusion.4
  76.2 2.9 gather_fusion.2
  79.1 1.4 fusion.56
  80.5 1.1 exponential_reduce_fusion.4
  84.6 2.9 gather_fusion.2
  87.6 1.3 fusion.56
  88.9 1.1 exponential_reduce_fusion.4
  93.0 2.9 gather_fusion.2
  96.0 1.4 fusion.56
  97.3 1.1 exponential_reduce_fusion.4
  101.4 2.9 gather_fusion.2
  104.4 1.4 fusion.56
  105.8 1.1 exponential_reduce_fusion.4
  109.9 2.9 gather_fusion.2
  112.8 1.3 fusion.56
  114.2 1.1 exponential_reduce_fusion.4
  116.9 31.7 %all-gather = f32[8,1,16384]{2,1,0:T(1,128)S(1)} all-gather(f32[1,1,16384]{2,1,0:T(1,128)S(1)} %reshape.154), channel_id=1, replica_groups=mesh['src'=8,'tgt'=4] {'src'}, dimensions={0}, use_global_device_ids=true | all-gather | bytes 589824 | tf_op jit(solution)/shard_map/all_gather | solution.py:12
  149.0 31.7 %all-gather.1 = f32[8,1,16384]{2,1,0:T(1,128)S(1)} all-gather(f32[1,1,16384]{2,1,0:T(1,128)S(1)} %reshape.156), channel_id=1, replica_groups=mesh['src'=8,'tgt'=4] {'src'}, dimensions={0}, use_global_device_ids=true | all-gather | bytes 589824 | tf_op jit(solution)/shard_map/all_gather | solution.py:12
  181.1 1.4 while.40
  183.1 90.2 %while.41 = (s32[]{:T(128)}, f32[32,256]{1,0:T(8,128)S(1)}, s32[]{:T(128)}, s32[640]{0:T(1024)S(1)}, pred[640]{0:T(1024)(128)(4,1)S(1)}, /*index=5*/f32[32,256]{...) while((s32[]{:T(128)}, f32[32,256]{1,0:T(8,128)S(1)}, ...), condition=%wide.region_13.14_spmd, body=%wide.region_10.13_spmd.sunk | while | flops 138418288 | bytes 3319143 | solution.py:115
  184.6 3.8 %gather_fusion.4 = bf16[16,256,64]{2,1,0:T(8,128)(2,1)} fusion(bf16[64,256,64]{2,1,0:T(8,128)(2,1)} %get-tuple-element.642, s32[1024]{0:T(1024)S(1)} %pad_clamp_fusion.15), kind=kCustom, calls=%fused_computation.6.clone.1 | custom fusion | bytes 1048640 | tf_op jit(solution)/shard_map/while/body/gather | solution.py:29
  189.0 2.3 exponential_reduce_fusion.5
  193.6 3.8 %gather_fusion.4 = bf16[16,256,64]{2,1,0:T(8,128)(2,1)} fusion(bf16[64,256,64]{2,1,0:T(8,128)(2,1)} %get-tuple-element.642, s32[1024]{0:T(1024)S(1)} %pad_clamp_fusion.15), kind=kCustom, calls=%fused_computation.6.clone.1 | custom fusion | bytes 1048640 | tf_op jit(solution)/shard_map/while/body/gather | solution.py:29
  198.0 2.3 exponential_reduce_fusion.5
  202.6 3.8 %gather_fusion.4 = bf16[16,256,64]{2,1,0:T(8,128)(2,1)} fusion(bf16[64,256,64]{2,1,0:T(8,128)(2,1)} %get-tuple-element.642, s32[1024]{0:T(1024)S(1)} %pad_clamp_fusion.15), kind=kCustom, calls=%fused_computation.6.clone.1 | custom fusion | bytes 1048640 | tf_op jit(solution)/shard_map/while/body/gather | solution.py:29
  207.0 2.3 exponential_reduce_fusion.5
  211.6 3.8 %gather_fusion.4 = bf16[16,256,64]{2,1,0:T(8,128)(2,1)} fusion(bf16[64,256,64]{2,1,0:T(8,128)(2,1)} %get-tuple-element.642, s32[1024]{0:T(1024)S(1)} %pad_clamp_fusion.15), kind=kCustom, calls=%fused_computation.6.clone.1 | custom fusion | bytes 1048640 | tf_op jit(solution)/shard_map/while/body/gather | solution.py:29
  216.1 2.3 exponential_reduce_fusion.5
  220.6 3.8 %gather_fusion.4 = bf16[16,256,64]{2,1,0:T(8,128)(2,1)} fusion(bf16[64,256,64]{2,1,0:T(8,128)(2,1)} %get-tuple-element.642, s32[1024]{0:T(1024)S(1)} %pad_clamp_fusion.15), kind=kCustom, calls=%fused_computation.6.clone.1 | custom fusion | bytes 1048640 | tf_op jit(solution)/shard_map/while/body/gather | solution.py:29
  225.1 2.3 exponential_reduce_fusion.5
  229.7 3.8 %gather_fusion.4 = bf16[16,256,64]{2,1,0:T(8,128)(2,1)} fusion(bf16[64,256,64]{2,1,0:T(8,128)(2,1)} %get-tuple-element.642, s32[1024]{0:T(1024)S(1)} %pad_clamp_fusion.15), kind=kCustom, calls=%fused_computation.6.clone.1 | custom fusion | bytes 1048640 | tf_op jit(solution)/shard_map/while/body/gather | solution.py:29
  234.1 2.3 exponential_reduce_fusion.5
  238.7 3.8 %gather_fusion.4 = bf16[16,256,64]{2,1,0:T(8,128)(2,1)} fusion(bf16[64,256,64]{2,1,0:T(8,128)(2,1)} %get-tuple-element.642, s32[1024]{0:T(1024)S(1)} %pad_clamp_fusion.15), kind=kCustom, calls=%fused_computation.6.clone.1 | custom fusion | bytes 1048640 | tf_op jit(solution)/shard_map/while/body/gather | solution.py:29
  243.1 2.3 exponential_reduce_fusion.5
  247.7 3.8 %gather_fusion.4 = bf16[16,256,64]{2,1,0:T(8,128)(2,1)} fusion(bf16[64,256,64]{2,1,0:T(8,128)(2,1)} %get-tuple-element.642, s32[1024]{0:T(1024)S(1)} %pad_clamp_fusion.15), kind=kCustom, calls=%fused_computation.6.clone.1 | custom fusion | bytes 1048640 | tf_op jit(solution)/shard_map/while/body/gather | solution.py:29
  252.1 2.3 exponential_reduce_fusion.5
  256.7 3.8 %gather_fusion.4 = bf16[16,256,64]{2,1,0:T(8,128)(2,1)} fusion(bf16[64,256,64]{2,1,0:T(8,128)(2,1)} %get-tuple-element.642, s32[1024]{0:T(1024)S(1)} %pad_clamp_fusion.15), kind=kCustom, calls=%fused_computation.6.clone.1 | custom fusion | bytes 1048640 | tf_op jit(solution)/shard_map/while/body/gather | solution.py:29
  261.1 2.3 exponential_reduce_fusion.5
  265.7 3.8 %gather_fusion.4 = bf16[16,256,64]{2,1,0:T(8,128)(2,1)} fusion(bf16[64,256,64]{2,1,0:T(8,128)(2,1)} %get-tuple-element.642, s32[1024]{0:T(1024)S(1)} %pad_clamp_fusion.15), kind=kCustom, calls=%fused_computation.6.clone.1 | custom fusion | bytes 1048640 | tf_op jit(solution)/shard_map/while/body/gather | solution.py:29
  270.1 2.3 exponential_reduce_fusion.5
  273.3 10.3 %all-reduce = f32[8192]{0:T(1024)S(1)} all-reduce(f32[8192]{0:T(1024)S(1)} %bitcast.147), channel_id=2, replica_groups=mesh['src'=8,'tgt'=4] {'tgt'}, use_global_device_ids=true, to_apply=%region_14.15.clone | all-reduce | flops 8192 | bytes 65536
  284.2 6.0 %all-reduce.2 = (f32[8]{0:T(128)S(1)}, f32[8,8]{1,0:T(8,128)S(1)}, f32[8,8]{1,0:T(8,128)S(1)}, f32[8]{0:T(128)S(1)}) all-reduce(f32[8]{0:T(128)S(1)} %convolution_bitcast_fusion.2, f32[8,8]{1,0:T(8,128)S(1)} %fusion.29, f32[8,8]{1,0:T(8,128)S(1)} %fusion.30, ...), channel_id=1, replica_groups=mesh['src'=8,'tgt'=4] {'tgt'}, use_global_device_ids=true, to_apply=%region_19.20 | all-reduce | flops 144 | bytes 1152 | tf_op jit(solution)/shard_map/psum | solution.py:126
  290.2 17.6 %all-reduce.1 = (f32[8]{0:T(128)S(1)}, f32[8,8]{1,0:T(8,128)S(1)}, f32[8,8]{1,0:T(8,128)S(1)}, f32[8]{0:T(128)S(1)}) all-reduce(f32[8]{0:T(128)S(1)} %get-tuple-element.297, f32[8,8]{1,0:T(8,128)S(1)} %get-tuple-element.298, f32[8,8]{1,0:T(8,128)S(1)} %get-tuple-element.299, ...), channel_id=1, replica_groups=mesh['src'=8,'tgt'=4] {'src'}, use_global_device_ids=true, to_apply=%region_20.21 | all-reduce | flops 144 | bytes 1152 | tf_op jit(solution)/shard_map/psum | solution.py:125
  (301 shorter events, 71.4 us)
Async XLA Ops:
  7.2 19.2 %copy-start = (f32[8,2048]{1,0:T(8,128)S(1)}, f32[8,2048]{1,0:T(8,128)}, u32[]{:S(2)}) copy-start(f32[8,2048]{1,0:T(8,128)} %param.19) | copy-start | bytes 196612
  7.2 8.7 %copy-start.5 = (f32[8192]{0:T(1024)S(1)}, f32[8192]{0:T(1024)}, u32[]{:S(2)}) copy-start(f32[8192]{0:T(1024)} %param.15) | copy-start | bytes 98308
  7.2 23.4 %all-gather.4.cloned.1.call-start = ((), (), s32[]{:S(2)}) async-start(), calls=%async_computation | async-start | bytes 1310720 | tf_op jit(solution)/shard_map/all_gather | solution.py:55
  11.0 12.8 %copy-start.6 = (u32[32]{0:T(128)S(1)}, u32[32]{0:T(128)}, u32[]{:S(2)}) copy-start(u32[32]{0:T(128)} %constant.169) | copy-start | bytes 388
  11.0 15.5 %copy-start.3 = (f32[8,2048]{1,0:T(8,128)S(1)}, f32[8,2048]{1,0:T(8,128)}, u32[]{:S(2)}) copy-start(f32[8,2048]{1,0:T(8,128)} %param.18) | copy-start | bytes 196612
  32.7 1.5 copy-start.1
  38.5 2.6 copy-start.2
  41.1 1.5 copy-start.1
  46.9 2.6 copy-start.2
  49.5 1.5 copy-start.1
  55.3 2.6 copy-start.2
  57.9 1.5 copy-start.1
  63.7 2.6 copy-start.2
  66.3 1.5 copy-start.1
  72.1 2.6 copy-start.2
  74.7 1.5 copy-start.1
  80.5 2.6 copy-start.2
  83.2 1.5 copy-start.1
  88.9 2.6 copy-start.2
  91.6 1.5 copy-start.1
  97.3 2.6 copy-start.2
  100.0 1.5 copy-start.1
  105.7 2.6 copy-start.2
  108.4 1.5 copy-start.1
  114.2 2.6 copy-start.2
  283.6 86.6 %copy-start.4 = (f32[2048]{0:T(1024)}, f32[2048]{0:T(1024)S(1)}, u32[]{:S(2)}) copy-start(f32[2048]{0:T(1024)S(1)} %dynamic-slice_subtract_fusion) | copy-start | bytes 24580
Sparse Core Ops, SparseCore 0:
  9.6 21.0 all-gather.3
